TPU v7x, 256 devices: a 8x8x2 block of a 8x8x16 slice. The times are simulated.
256 devices in a mesh: groups: 2 (over z), owner: 128 (over y, x, core).
Axes of the slice: x: 8, y: 8, z: 2, core: 2. Of those that a mesh axis runs over, the one named last changes fastest.
The devices are a block of a 8x8x16 slice.
Arguments:
- queries: bfloat16 [16384, 1024], P(('groups', 'owner')), parts along dimension 0, may hold values from -0.3984375 to 0.3984375
- probes: int32 [16384, 8], P(('groups', 'owner')), parts along dimension 0, may hold values from 0 to 2047, as said below
- passages: bfloat16 [2048, 256, 1024], P('owner'), may hold values from -6 to 6
- centroids: bfloat16 [2048, 1024], P('owner'), may hold values from -6 to 6
- counts: int32 [2048], P('owner'), may hold values from 1 to 256
Outputs:
- scores: float32 [16384, 8, 256], P(('groups', 'owner')), parts along dimension 0
- visits: int32 [16384], P(('groups', 'owner')), parts along dimension 0
There are 2 independent parts, one for each index of `groups`. A program takes and returns all parts, laid end to end along the dimension named above; an argument that names none is the same for every part. Nothing has to cross between parts.
Inputs may be any that keep to these rules, and one draw needn't show every extreme that they name: Cluster c belongs to owner index c // 16. In each aligned block of 64 queries (the queries of one index of owner) at most 8 probes name clusters of one owner, and in every draw some owners receive exactly 8 probes from every block. A query may name a cluster more than once.
All inputs are finite; a program needn't handle non-finite values.
Results may differ from a plain program's by a relative error of at most 0.0003.
Values may be sent and summed in bfloat16 or wider, within the bound.
A program may use at most 64 MiB of HBM per device.

v0:
```python
import jax
import jax.numpy as jnp
from jax import lax
from jax.sharding import PartitionSpec as P


def body(queries, probes, passages, centroids, counts):
    owner_count = lax.axis_size("owner")
    per_device, probe_count = probes.shape
    local_count, block_span, feature_width = passages.shape
    capacity = 2 * per_device * probe_count // owner_count
    pair_count = per_device * probe_count
    passage_blocks = jnp.transpose(passages, (0, 2, 1))
    flat_probes = probes.reshape(-1)
    target_owner = flat_probes // local_count
    target_local = flat_probes % local_count
    owner_hits = (
        target_owner[:, None] == jnp.arange(owner_count, dtype=jnp.int32)[None, :]
    ).astype(jnp.int32)
    slot_rank = jnp.sum((jnp.cumsum(owner_hits, axis=0) - owner_hits) * owner_hits, axis=1)
    slot_index = target_owner * capacity + slot_rank
    pair_ids = jnp.arange(pair_count, dtype=jnp.int32)
    slot_match = slot_index[None, :] == jnp.arange(owner_count * capacity, dtype=jnp.int32)[:, None]
    slot_filled = jnp.any(slot_match, axis=1)
    source_pair = jnp.sum(jnp.where(slot_match, pair_ids[None, :], 0), axis=1)
    send_rows = jnp.where(
        slot_filled[:, None], queries[source_pair // probe_count], jnp.zeros((), jnp.bfloat16)
    )
    send_ids = jnp.where(slot_filled, target_local[source_pair], -1)
    query_rows = lax.all_to_all(
        send_rows.reshape(owner_count, capacity, feature_width),
        "owner",
        split_axis=0,
        concat_axis=0,
        tiled=True,
    )
    cluster_ids = lax.all_to_all(
        send_ids.reshape(owner_count, capacity), "owner", split_axis=0, concat_axis=0, tiled=True
    )
    source_count, slot_count = cluster_ids.shape
    row_total = source_count * slot_count
    flat_rows = query_rows.reshape(row_total, feature_width)
    flat_ids = cluster_ids.reshape(-1)
    group_ids = jnp.where(flat_ids < 0, 0, flat_ids).astype(jnp.int32)
    cluster_pick = flat_ids[:, None] == jnp.arange(local_count, dtype=jnp.int32)[None, :]
    live_sizes = jnp.sum(jnp.where(cluster_pick, counts[None, :], 0), axis=1)
    group_pick = group_ids[:, None] == jnp.arange(local_count, dtype=jnp.int32)[None, :]
    group_sizes = jnp.sum(group_pick.astype(jnp.int32), axis=0)
    order = jnp.argsort(group_ids, stable=True)
    undo_order = jnp.argsort(order, stable=True)
    sorted_rows = flat_rows[order]
    sorted_scores = lax.ragged_dot(
        sorted_rows, passage_blocks, group_sizes, preferred_element_type=jnp.float32
    )
    own_scores = sorted_scores[undo_order]
    centre_term = jnp.einsum(
        "rd,rd->r", flat_rows, centroids[group_ids], preferred_element_type=jnp.float32
    )
    live_mask = jnp.arange(block_span, dtype=jnp.int32)[None, :] < live_sizes[:, None]
    masked_scores = jnp.where(live_mask, own_scores + centre_term[:, None], 0.0)
    back_scores = lax.all_to_all(
        masked_scores.reshape(source_count, slot_count, block_span),
        "owner",
        split_axis=0,
        concat_axis=0,
        tiled=True,
    )
    back_sizes = lax.all_to_all(
        live_sizes.astype(jnp.float32).reshape(source_count, slot_count),
        "owner",
        split_axis=0,
        concat_axis=0,
        tiled=True,
    )
    flat_scores = back_scores.reshape(owner_count * capacity, block_span)
    scores = flat_scores[slot_index].reshape(per_device, probe_count, block_span)
    pair_sizes = back_sizes.reshape(-1)[slot_index].reshape(per_device, probe_count)
    visits = jnp.sum(pair_sizes, axis=1).astype(jnp.int32)
    return (scores, visits)


def solution(mesh):
    in_specs = (
        P(("groups", "owner"), None),
        P(("groups", "owner"), None),
        P("owner", None, None),
        P("owner", None),
        P("owner"),
    )
    out_specs = (P(("groups", "owner"), None, None), P(("groups", "owner")))
    return jax.shard_map(body, mesh=mesh, in_specs=in_specs, out_specs=out_specs, check_vma=False)
```

profile of v0, /device:TPU:513, one launch (start us, length us, event | category | flops | bytes accessed | tf_op | source)
XLA Modules:
  0.0 201.1 jit_solution(762799643791499349)
XLA Ops:
  0.6 0.8 copy.22
  2.6 0.3 select_reduce_fusion
  3.0 6.9 %gather_fusion = s32[1024]{0:T(1024)S(1)} fusion(s32[512]{0:T(512)S(1)} %get-tuple-element.12, s32[1024]{0:T(1024)S(1)} %broadcast_clamp_fusion.2), kind=kCustom, calls=%fused_computation | custom fusion | bytes 12288 | tf_op jit(solution)/shard_map/gather | solution.py:29
  9.9 0.7 select_n.145
  10.6 27.4 %all-to-all-start = ((s32[128,1,8]{2,1,0:T(1,128)}), s32[128,1,8]{2,1,0:T(1,128)S(1)}, u32[]{:S(2)}, u32[]{:S(2)}) async-start(s32[128,1,8]{2,1,0:T(1,128)} %bitcast.5), calls=%async_computation | async-start | bytes 131072 | tf_op jit(solution)/shard_map/all_to_all | solution.py:37
  38.1 4.1 %gather_fusion.1 = bf16[1024,1024]{1,0:T(8,128)(2,1)S(1)} fusion(bf16[64,1024]{1,0:T(8,128)(2,1)S(1)} %copy-done, s32[1024]{0:T(1024)S(1)} %broadcast_clamp_fusion.1), kind=kCustom, calls=%fused_computation.1 | custom fusion | bytes 4198400 | tf_op jit(solution)/shard_map/gather | solution.py:27
  42.2 1.6 bitcast_select_fusion
  43.8 6.4 %all-to-all-done = s32[128,1,8]{2,1,0:T(1,128)S(1)} async-done(((s32[128,1,8]{2,1,0:T(1,128)}), s32[128,1,8]{2,1,0:T(1,128)S(1)}, u32[]{:S(2)}, u32[]{:S(2)}) %all-to-all-start) | async-done | bytes 4128 | tf_op jit(solution)/shard_map/all_to_all | solution.py:37
  50.2 10.2 %all-to-all-start.1 = ((bf16[128,8,1024]{2,1,0:T(8,128)(2,1)}), bf16[128,8,1024]{2,1,0:T(8,128)(2,1)S(1)}, u32[]{:S(2)}, u32[]{:S(2)}) async-start(bf16[128,8,1024]{2,1,0:T(8,128)(2,1)} %bitcast_select_fusion), calls=%async_computation.1 | async-start | bytes 4194304 | tf_op jit(solution)/shard_map/all_to_all | solution.py:30
  60.4 12.3 %copy.27 = bf16[16,256,1024]{1,2,0:T(8,128)(2,1)} copy(bf16[16,256,1024]{2,1,0:T(8,128)(2,1)} %param.7) | data formatting | bytes 16777216 | tf_op args[2]
  72.7 0.5 broadcast.356
  73.2 0.8 reduce.10
  74.4 4.4 %sort.31 = (s32[1024]{0:T(1024)}, s32[1024]{0:T(1024)S(1)}) sort(s32[1024]{0:T(1024)S(1)} %compare_select_fusion.6, s32[1024]{0:T(1024)S(1)} %iota.35), dimensions={0}, to_apply=%region_6.7 | sort | flops 10240 | bytes 16384 | tf_op jit(solution)/shard_map/jit(argsort)/sort | solution.py:49
  78.8 0.6 convert_reduce_fusion
  79.4 1.8 ragged-dot-metadata
  81.2 0.7 convert_element_type.31
  82.0 4.4 %sort.32 = (s32[1024]{0:T(1024)}, s32[1024]{0:T(1024)S(1)}) sort(s32[1024]{0:T(1024)S(1)} %get-tuple-element.4, s32[1024]{0:T(1024)S(1)} %iota.36), dimensions={0}, to_apply=%region_8.9 | sort | flops 10240 | bytes 16384 | tf_op jit(solution)/shard_map/jit(argsort)/sort | solution.py:50
  86.4 5.4 %gather_fusion.4 = bf16[1024,1024]{1,0:T(8,128)(2,1)} fusion(bf16[16,1024]{1,0:T(8,128)(2,1)S(1)} %copy-done.1, s32[1024]{0:T(1024)S(1)} %broadcast_clamp_fusion), kind=kCustom, calls=%fused_computation.4 | custom fusion | bytes 4198400 | tf_op jit(solution)/shard_map/gather | solution.py:57
  91.7 19.2 %all-to-all-done.1 = bf16[128,8,1024]{2,1,0:T(8,128)(2,1)S(1)} async-done(((bf16[128,8,1024]{2,1,0:T(8,128)(2,1)}), bf16[128,8,1024]{2,1,0:T(8,128)(2,1)S(1)}, u32[]{:S(2)}, u32[]{:S(2)}) %all-to-all-start.1) | async-done | bytes 2097184 | tf_op jit(solution)/shard_map/all_to_all | solution.py:30
  111.0 10.6 %all-to-all-start.3 = ((f32[128,1,8]{2,1,0:T(1,128)}), f32[128,1,8]{2,1,0:T(1,128)S(1)}, u32[]{:S(2)}, u32[]{:S(2)}) async-start(f32[128,1,8]{2,1,0:T(1,128)} %bitcast.16), calls=%async_computation.3 | async-start | bytes 131072 | tf_op jit(solution)/shard_map/all_to_all | solution.py:68
  121.6 2.2 %fusion = f32[1024]{0:T(1024)S(1)} fusion(bf16[1024,1024]{1,0:T(8,128)(2,1)} %gather_fusion.4, bf16[128,8,1024]{2,1,0:T(8,128)(2,1)S(1)} %all-to-all-done.1), kind=kLoop, calls=%fused_computation.8 | loop fusion | flops 4193280 | bytes 4198400 | tf_op jit(solution)/shard_map/rd,rd->r/dot_general | solution.py:56
  123.9 5.4 %gather_fusion.2 = bf16[1024,1024]{1,0:T(8,128)(2,1)} fusion(bf16[1024,1024]{1,0:T(8,128)(2,1)S(1)} %bitcast.33, s32[1024]{0:T(1024)S(1)} %fusion.8), kind=kCustom, calls=%fused_computation.2 | custom fusion | bytes 4198400 | tf_op jit(solution)/shard_map/gather | solution.py:51
  129.3 17.0 %ragged-dot-none = f32[1024,256]{1,0:T(8,128)} custom-call(s32[1]{0:T(128)} %get-tuple-element.6, s32[17]{0:T(128)} %get-tuple-element.7, s32[19]{0:T(128)} %get-tuple-element.8, s32[19]{0:T(128)} %get-tuple-element.9, s32[1]{0:T(128)} %get-tuple-element.6, bf16[1024,1024]{1,0:T(8,128)(2,1)} %gather_fusion.2, bf16[16,1024,256]{2,1,0:T(8,128)(2,1)} %bitcast.34), custom_call_target="tpu_custom_call" | custom-call | flops 536870912 | bytes 11534400 | tf_op jit(solution)/shard_map/ragged_dot_general/ragged-dot-none
  146.3 4.7 %gather_fusion.3 = f32[1024,256]{1,0:T(8,128)S(1)} fusion(f32[1024,256]{1,0:T(8,128)} %ragged-dot-none, s32[1024]{0:T(1024)S(1)} %fusion.9), kind=kCustom, calls=%fused_computation.3 | custom fusion | bytes 2101248 | tf_op jit(solution)/shard_map/gather | solution.py:55
  151.0 1.3 fusion.2
  152.4 16.4 %all-to-all-start.2 = ((f32[128,8,256]{2,1,0:T(8,128)}), f32[128,8,256]{2,1,0:T(8,128)S(1)}, u32[]{:S(2)}, u32[]{:S(2)}) async-start(f32[128,8,256]{2,1,0:T(8,128)} %fusion.2), calls=%async_computation.2 | async-start | bytes 2097152 | tf_op jit(solution)/shard_map/all_to_all | solution.py:61
  168.9 0.5 broadcast.357
  169.4 0.8 reduce.11
  170.3 2.3 %gather_fusion.6 = f32[512]{0:T(512)S(1)} fusion(f32[1024]{0:T(1024)S(1)} %reshape.359, s32[1024]{0:T(1024)S(1)} %pad_clamp_fusion), kind=kCustom, calls=%fused_computation.6 | custom fusion | bytes 6144 | tf_op jit(solution)/shard_map/gather | solution.py:77
  172.8 0.5 convert_element_type.32
  173.3 25.6 %all-to-all-done.2 = f32[128,8,256]{2,1,0:T(8,128)S(1)} async-done(((f32[128,8,256]{2,1,0:T(8,128)}), f32[128,8,256]{2,1,0:T(8,128)S(1)}, u32[]{:S(2)}, u32[]{:S(2)}) %all-to-all-start.2) | async-done | bytes 1048608 | tf_op jit(solution)/shard_map/all_to_all | solution.py:61
  198.9 2.2 %gather_fusion.5 = f32[512,256]{1,0:T(8,128)} fusion(f32[1024,256]{1,0:T(8,128)S(1)} %bitcast.35, s32[1024]{0:T(1024)S(1)} %pad_clamp_fusion), kind=kCustom, calls=%fused_computation.5 | custom fusion | bytes 1050624 | tf_op jit(solution)/shard_map/gather | solution.py:76
  (46 shorter events, 2.2 us)
Async XLA Ops:
  0.6 37.5 %copy-start = (bf16[64,1024]{1,0:T(8,128)(2,1)S(1)}, bf16[64,1024]{1,0:T(8,128)(2,1)}, u32[]{:S(2)}) copy-start(bf16[64,1024]{1,0:T(8,128)(2,1)} %param.5) | copy-start | bytes 393220
  10.6 39.7 %all-to-all-start = ((s32[128,1,8]{2,1,0:T(1,128)}), s32[128,1,8]{2,1,0:T(1,128)S(1)}, u32[]{:S(2)}, u32[]{:S(2)}) async-start(s32[128,1,8]{2,1,0:T(1,128)} %bitcast.5), calls=%async_computation | async-start | bytes 131072 | tf_op jit(solution)/shard_map/all_to_all | solution.py:37
  50.2 60.7 %all-to-all-start.1 = ((bf16[128,8,1024]{2,1,0:T(8,128)(2,1)}), bf16[128,8,1024]{2,1,0:T(8,128)(2,1)S(1)}, u32[]{:S(2)}, u32[]{:S(2)}) async-start(bf16[128,8,1024]{2,1,0:T(8,128)(2,1)} %bitcast_select_fusion), calls=%async_computation.1 | async-start | bytes 4194304 | tf_op jit(solution)/shard_map/all_to_all | solution.py:30
  60.4 13.7 %copy-start.2 = (s32[16]{0:T(128)S(1)}, s32[16]{0:T(128)}, u32[]{:S(2)}) copy-start(s32[16]{0:T(128)} %param.9) | copy-start | bytes 196
  72.7 13.6 %copy-start.1 = (bf16[16,1024]{1,0:T(8,128)(2,1)S(1)}, bf16[16,1024]{1,0:T(8,128)(2,1)}, u32[]{:S(2)}) copy-start(bf16[16,1024]{1,0:T(8,128)(2,1)} %param.8) | copy-start | bytes 98308
  111.0 41.4 %all-to-all-start.3 = ((f32[128,1,8]{2,1,0:T(1,128)}), f32[128,1,8]{2,1,0:T(1,128)S(1)}, u32[]{:S(2)}, u32[]{:S(2)}) async-start(f32[128,1,8]{2,1,0:T(1,128)} %bitcast.16), calls=%async_computation.3 | async-start | bytes 131072 | tf_op jit(solution)/shard_map/all_to_all | solution.py:68
  152.4 46.5 %all-to-all-start.2 = ((f32[128,8,256]{2,1,0:T(8,128)}), f32[128,8,256]{2,1,0:T(8,128)S(1)}, u32[]{:S(2)}, u32[]{:S(2)}) async-start(f32[128,8,256]{2,1,0:T(8,128)} %fusion.2), calls=%async_computation.2 | async-start | bytes 2097152 | tf_op jit(solution)/shard_map/all_to_all | solution.py:61
where the time goes:
time: 202 us; the launch traced here: 201 us
  starting transfers between devices  64.6 us (32%)
  waiting for transfers between devices  51.3 us (25%)
  local copies, waits for them, and re-layouts  47.5 us (24%)
  Pallas kernels  18.8 us (9%)
  other arithmetic  18 us (9%)
    all_to_all x1, starting transfers between devices, body(): lax.all_to_all(send_ids.reshape(owner_count, capacity), 'owner', split_ax...  27.4 us
    all_to_all x1, waiting for transfers between devices, body(): lax.all_to_all(masked_scores.reshape(source_count, slot_count, block_span...  25.6 us
    all_to_all x1, waiting for transfers between devices, body(): lax.all_to_all(send_rows.reshape(owner_count, capacity, feature_width), '...  19.2 us
    another operation x1, Pallas kernels  17 us
    all_to_all x1, starting transfers between devices, body(): lax.all_to_all(masked_scores.reshape(source_count, slot_count, block_span...  16.4 us
    unnamed x9, local copies, waits for them, and re-layouts  13.1 us
    all_to_all x1, starting transfers between devices, body(): lax.all_to_all(live_sizes.astype(jnp.float32).reshape(source_count, slot_...  10.6 us
    all_to_all x1, starting transfers between devices, body(): lax.all_to_all(send_rows.reshape(owner_count, capacity, feature_width), '...  10.2 us
  transfers between devices with their start and end apart: 4, of which 3 were waited for; matrix products, arithmetic and copies ran while one was open for 27% of the time, Pallas kernels for 9%

commit v1 on v0

v1 whole, which is shorter than its diff:
```python
import functools
import math

import jax
import jax.numpy as jnp
from jax import lax
from jax.experimental import pallas as pl
from jax.experimental.pallas import tpu as pltpu
from jax.sharding import PartitionSpec as P

MESH = pl.DeviceIdType.MESH
LANES = 128
CODE_TOP = 32767.0


def iota(shape, dim):
    return lax.broadcasted_iota(jnp.int32, shape, dim)


def shift_of(t):
    return (2 * lax.rem(t, 2) - 1) * lax.div(t + 1, 2)


def kernel(
    side,
    cap,
    q_hbm,
    pcol_ref,
    pass_hbm,
    cent_ref,
    cnt_ref,
    out_ref,
    vis_ref,
    gq,
    gcode,
    snd,
    scid,
    rcv,
    rcid,
    acc,
    rs,
    sm,
    ret,
    rmeta,
    pv,
    tgt,
    slot_ref,
    load_sem,
    pass_sem,
    gq_send,
    gq_recv,
    gc_send,
    gc_recv,
    x_send,
    x_recv,
    c_send,
    c_recv,
    b_send,
    b_recv,
    m_send,
    m_recv,
):
    me = lax.axis_index("owner")
    core = lax.rem(me, 2)
    x = lax.rem(lax.div(me, 2), side)
    y = lax.div(me, 2 * side)
    local_count, span, width = pv.shape
    per_device = gq.shape[1]
    pair_count = pcol_ref.shape[0]
    probe_count = pair_count // per_device
    owner_count = side * side * 2
    pairs = side // 2
    dests = side * 2
    rows = dests * 2 * cap

    def wrap(v):
        return lax.rem(v + side, side)

    def device(first, second, cls, dest_core):
        yy = wrap(y + second * (1 - cls) + first * cls)
        xx = wrap(x + first * (1 - cls) + second * cls)
        return {"owner": (yy * side + xx) * 2 + dest_core}

    def remote(src, dst, send, recv, dev):
        return pltpu.make_async_remote_copy(
            src_ref=src, dst_ref=dst, send_sem=send, recv_sem=recv, device_id=dev, device_id_type=MESH
        )

    own_q = pltpu.make_async_copy(q_hbm, gq.at[0], load_sem)
    own_q.start()
    own_p = pltpu.make_async_copy(pass_hbm, pv, pass_sem)
    own_p.start()

    barrier = pltpu.get_barrier_semaphore()

    def greet(t, carry):
        for dest_core in range(2):
            for axis in range(2):
                pl.semaphore_signal(
                    barrier, inc=1, device_id=device(0, shift_of(t), axis, dest_core), device_id_type=MESH
                )
        return carry

    lax.fori_loop(1, side, greet, 0)
    pl.semaphore_signal(barrier, inc=1, device_id=device(0, 0, 0, 1 - core), device_id_type=MESH)

    pcol = pcol_ref[...]
    owner_col = lax.div(pcol, local_count)
    hits = (owner_col == iota((pair_count, owner_count), 1)).astype(jnp.float32)
    earlier = (iota((pair_count, pair_count), 0) > iota((pair_count, pair_count), 1)).astype(jnp.float32)
    before = jnp.dot(
        earlier.astype(jnp.bfloat16), hits.astype(jnp.bfloat16), preferred_element_type=jnp.float32
    )
    rank = jnp.sum(hits * before, axis=1, keepdims=True).astype(jnp.int32)
    slot_col = owner_col * cap + rank
    slot_ref[...] = slot_col
    code_col = slot_col * local_count + lax.rem(pcol, local_count)
    lane = iota((pair_count, LANES), 1)
    at_lane = lax.rem(lane, per_device) == lax.div(iota((pair_count, LANES), 0), probe_count)
    gcode[0] = jnp.sum(jnp.where(at_lane, code_col, 0).reshape(per_device, probe_count, LANES), axis=0)

    row = iota((rows, LANES), 0)
    dest = lax.div(row, 2 * cap)
    second = shift_of(lax.div(dest, 2))
    yy = wrap(y + second * (1 - core))
    xx = wrap(x + second * core)
    row_slot = ((yy * side + xx) * 2 + lax.rem(dest, 2)) * cap + lax.rem(row, cap)
    mine = lax.rem(lax.div(row, cap), 2) == lax.div(iota((rows, LANES), 1), per_device)
    tgt[...] = jnp.where(mine, row_slot, -1)

    own_q.wait()
    pl.semaphore_wait(barrier, 4 * (side - 1) + 1)

    def share(t, carry):
        dev = device(shift_of(t), 0, core, core)
        remote(gcode.at[0], gcode.at[t], gc_send.at[t], gc_recv.at[t], dev).start()
        remote(gq.at[0], gq.at[t], gq_send.at[t], gq_recv.at[t], dev).start()
        return carry

    lax.fori_loop(1, side, share, 0)

    def to_owner(p, f, dest_core):
        dev = device(0, shift_of(f), core, dest_core)
        d = f * 2 + dest_core
        return (
            remote(snd.at[p, d], rcv.at[p, f * 2 + core], x_send.at[p], x_recv.at[p], dev),
            remote(scid.at[p, d], rcid.at[p, f * 2 + core], c_send.at[p], c_recv.at[p], dev),
        )

    for p in range(pairs):
        for t in (2 * p, 2 * p + 1):
            if t:
                dev = device(0, 0, core, core)
                remote(gcode.at[0], gcode.at[t], gc_send.at[t], gc_recv.at[t], dev).wait_recv()
                remote(gq.at[0], gq.at[t], gq_send.at[t], gq_recv.at[t], dev).wait_recv()
        code = jnp.where(iota((probe_count, LANES), 1) < per_device, gcode[2 * p], gcode[2 * p + 1])
        slot_of = lax.div(code, local_count)
        mark_of = (lax.rem(code, local_count) + 1).astype(jnp.float32)
        target = tgt[...]
        mark = jnp.zeros((rows, LANES), jnp.float32)
        for j in range(probe_count):
            mark = jnp.where(target == slot_of[j : j + 1, :], mark_of[j : j + 1, :], mark)
        pick = jnp.where(mark > 0.0, 1.0, 0.0).astype(jnp.bfloat16)
        step = 256
        for n in range(0, width, step):
            part = gq[2 * p : 2 * p + 2, :, n : n + step].reshape(2 * per_device, step)
            took = jnp.dot(pick, part, preferred_element_type=jnp.float32)
            snd[p, :, :, n : n + step] = took.astype(jnp.bfloat16).reshape(dests, 2 * cap, step)
        mark_col = jnp.sum(mark, axis=1, keepdims=True)
        spot = iota((rows, LANES), 1) == lax.rem(iota((rows, LANES), 0), 2 * cap)
        marks = jnp.sum(jnp.where(spot, mark_col, 0.0).reshape(dests, 2 * cap, LANES), axis=1)
        for d in range(dests):
            scid[p, d] = marks[d : d + 1, :]

        self_x = pltpu.make_async_copy(snd.at[p, core], rcv.at[p, core], x_recv.at[p])
        self_c = pltpu.make_async_copy(scid.at[p, core], rcid.at[p, core], c_recv.at[p])
        self_c.start()
        self_x.start()
        for copy in to_owner(p, 0, 1 - core):
            copy.start()

        def post(f, carry):
            for dest_core in range(2):
                a, b = to_owner(p, f, dest_core)
                b.start()
                a.start()
            return carry

        lax.fori_loop(1, side, post, 0)

    def whole(ref, sem):
        return pltpu.make_async_copy(ref, ref, sem)

    own_p.wait()

    def back(p, f, cls, i):
        t = 2 * p + i
        dev = device(-shift_of(t), -shift_of(f), cls, cls)
        b = (f * 2 + cls) * 2 + i
        land = (f * 2 + core) * 2 + i
        return (
            remote(sm.at[p, b], rmeta.at[p, land], m_send.at[p], m_recv.at[p], dev),
            remote(rs.at[p, b], ret.at[p, land], b_send.at[p], b_recv.at[p], dev),
        )

    for p in range(pairs):
        whole(rcid.at[p], c_recv.at[p]).wait()
        whole(rcv.at[p], x_recv.at[p]).wait()
        row = iota((rows, LANES), 0)
        lane = iota((rows, LANES), 1)
        seen = jnp.broadcast_to(rcid[p], (dests, 2 * cap, LANES)).reshape(rows, LANES)
        cid = jnp.sum(jnp.where(lane == lax.rem(row, 2 * cap), seen, 0.0), axis=1, keepdims=True) - 1.0
        cid = cid.astype(jnp.int32)
        acc[...] = jnp.zeros_like(acc)

        def cluster(c, carry):
            got = lax.dot_general(
                rcv[p].reshape(rows, width),
                pv[c],
                (((1,), (1,)), ((), ())),
                preferred_element_type=jnp.float32,
            )
            acc[...] = jnp.where(cid == c, got, acc[...])
            return carry

        lax.fori_loop(0, local_count, cluster, 0)
        centres = lax.dot_general(
            rcv[p].reshape(rows, width),
            cent_ref[...],
            (((1,), (1,)), ((), ())),
            preferred_element_type=jnp.float32,
        )
        of_row = iota((rows, local_count), 1) == cid
        centre = jnp.sum(jnp.where(of_row, centres, 0.0), axis=1, keepdims=True)
        live = jnp.sum(jnp.where(of_row, cnt_ref[...], 0.0), axis=1, keepdims=True)
        within = iota((rows, span), 1).astype(jnp.float32) < live
        value = jnp.where(within, acc[...] + centre, 0.0)
        top = jnp.maximum(jnp.max(jnp.abs(value), axis=1, keepdims=True), 1e-30)
        coded = jnp.round(value * (CODE_TOP / top)).astype(jnp.int32)
        low, high = coded[:, : span // 2], coded[:, span // 2 :]
        rs[p] = (high * 65536 + (low & 65535)).reshape(dests * 2, cap, LANES)
        spot = lax.rem(lane, cap) == lax.rem(row, cap)
        scales = jnp.sum(
            jnp.where(spot, top * (1.0 / CODE_TOP), 0.0).reshape(dests * 2, cap, LANES), axis=1
        )
        lives = jnp.sum(jnp.where(spot, live, 0.0).reshape(dests * 2, cap, LANES), axis=1)
        both = jnp.concatenate([scales, lives], axis=1)
        for b in range(dests * 2):
            sm[p, b] = both[b : b + 1, :]

        def give(f, carry):
            for cls in range(2):
                for i in range(2):
                    for copy in back(p, f, cls, i):
                        copy.start()
            return carry

        if p == 0:
            self_b = core * 2
            pltpu.make_async_copy(sm.at[0, self_b], rmeta.at[0, self_b], m_recv.at[0]).start()
            pltpu.make_async_copy(rs.at[0, self_b], ret.at[0, self_b], b_recv.at[0]).start()
            for copy in back(0, 0, 1 - core, 0):
                copy.start()
            for cls in range(2):
                for copy in back(0, 0, cls, 1):
                    copy.start()
            lax.fori_loop(1, side, give, 0)
        else:
            lax.fori_loop(0, side, give, 0)

    scale_col = jnp.zeros((pair_count, 1), jnp.float32)
    live_col = jnp.zeros((pair_count, 1), jnp.float32)
    slots = slot_ref[...]
    for p in range(pairs):
        whole(rmeta.at[p], m_recv.at[p]).wait()
        whole(ret.at[p], b_recv.at[p]).wait()
        spot_lane = iota((1, rows), 1)
        block = lax.div(spot_lane, cap)
        second = shift_of(lax.div(block, 4))
        first = shift_of(2 * p + lax.rem(block, 2))
        yy = wrap(y + second * (1 - core) + first * core)
        xx = wrap(x + first * (1 - core) + second * core)
        have = ((yy * side + xx) * 2 + lax.rem(lax.div(block, 2), 2)) * cap + lax.rem(spot_lane, cap)
        match = slots == have
        pick = jnp.where(match, 1.0, 0.0).astype(jnp.bfloat16)
        words = ret[p].reshape(rows, LANES)

        def piece(low, high):
            return jnp.concatenate([low, high], axis=1).astype(jnp.float32).astype(jnp.bfloat16)

        tops = piece(
            lax.shift_right_arithmetic(lax.shift_left(words, 16), 24), lax.shift_right_arithmetic(words, 24)
        )
        tails = piece(words & 255, lax.shift_right_arithmetic(words, 16) & 255)
        sums = 256.0 * jnp.dot(pick, tops, preferred_element_type=jnp.float32) + jnp.dot(
            pick, tails, preferred_element_type=jnp.float32
        )
        out_ref[...] = sums if p == 0 else out_ref[...] + sums
        each = LANES // cap
        scale_lane, live_lane = [], []
        for h in range(rows // LANES):
            meta = jnp.concatenate([rmeta[p, h * each + b] for b in range(each)], axis=0)
            keep = lax.div(iota((each, LANES), 1), cap) == iota((each, LANES), 0)
            scale_lane.append(jnp.sum(jnp.where(keep, meta[:, :LANES], 0.0), axis=0, keepdims=True))
            live_lane.append(jnp.sum(jnp.where(keep, meta[:, LANES:], 0.0), axis=0, keepdims=True))
        scale_col += jnp.sum(
            jnp.where(match, jnp.concatenate(scale_lane, axis=1), 0.0), axis=1, keepdims=True
        )
        live_col += jnp.sum(jnp.where(match, jnp.concatenate(live_lane, axis=1), 0.0), axis=1, keepdims=True)
    out_ref[...] = out_ref[...] * scale_col
    at_query = iota((pair_count, LANES), 1) == lax.div(iota((pair_count, LANES), 0), probe_count)
    vis_ref[...] = jnp.sum(jnp.where(at_query, live_col, 0.0), axis=0, keepdims=True).astype(jnp.int32)

    def sent(t, carry):
        dev = device(shift_of(t), 0, core, core)
        remote(gcode.at[0], gcode.at[t], gc_send.at[t], gc_recv.at[t], dev).wait_send()
        remote(gq.at[0], gq.at[t], gq_send.at[t], gq_recv.at[t], dev).wait_send()
        return carry

    lax.fori_loop(1, side, sent, 0)
    for p in range(pairs):
        whole(snd.at[p, pl.ds(0, dests - 1)], x_send.at[p]).wait()
        whole(scid.at[p, pl.ds(0, dests - 1)], c_send.at[p]).wait()
        blocks = dests * 2 - (1 if p == 0 else 0)
        whole(rs.at[p, pl.ds(0, blocks)], b_send.at[p]).wait()
        whole(sm.at[p, pl.ds(0, blocks)], m_send.at[p]).wait()


def body(queries, probes, passages, centroids, counts):
    owner_count = lax.axis_size("owner")
    side = math.isqrt(owner_count // 2)
    per_device, probe_count = probes.shape
    local_count, span, width = passages.shape
    pair_count = per_device * probe_count
    cap = 2 * pair_count // owner_count
    pairs = side // 2
    dests = side * 2
    rows = dests * 2 * cap
    vmem = pl.BlockSpec(memory_space=pltpu.VMEM)
    hbm = pl.BlockSpec(memory_space=pl.ANY)
    dma = pltpu.SemaphoreType.DMA
    scores, visits = pl.pallas_call(
        functools.partial(kernel, side, cap),
        out_shape=(
            jax.ShapeDtypeStruct((pair_count, span), jnp.float32),
            jax.ShapeDtypeStruct((1, LANES), jnp.int32),
        ),
        in_specs=[hbm, vmem, hbm, vmem, vmem],
        out_specs=(vmem, vmem),
        scratch_shapes=[
            pltpu.VMEM((side, per_device, width), jnp.bfloat16),
            pltpu.VMEM((side, probe_count, LANES), jnp.int32),
            pltpu.VMEM((pairs, dests, 2 * cap, width), jnp.bfloat16),
            pltpu.VMEM((pairs, dests, 1, LANES), jnp.float32),
            pltpu.VMEM((pairs, dests, 2 * cap, width), jnp.bfloat16),
            pltpu.VMEM((pairs, dests, 1, LANES), jnp.float32),
            pltpu.VMEM((rows, span), jnp.float32),
            pltpu.VMEM((pairs, dests * 2, cap, LANES), jnp.int32),
            pltpu.VMEM((pairs, dests * 2, 1, 2 * LANES), jnp.float32),
            pltpu.VMEM((pairs, dests * 2, cap, LANES), jnp.int32),
            pltpu.VMEM((pairs, dests * 2, 1, 2 * LANES), jnp.float32),
            pltpu.VMEM((local_count, span, width), jnp.bfloat16),
            pltpu.VMEM((rows, LANES), jnp.int32),
            pltpu.VMEM((pair_count, 1), jnp.int32),
            dma,
            dma,
            dma((side,)),
            dma((side,)),
            dma((side,)),
            dma((side,)),
            dma((pairs,)),
            dma((pairs,)),
            dma((pairs,)),
            dma((pairs,)),
            dma((pairs,)),
            dma((pairs,)),
            dma((pairs,)),
            dma((pairs,)),
        ],
        compiler_params=pltpu.CompilerParams(
            collective_id=0, has_side_effects=True, vmem_limit_bytes=48 * 1024 * 1024
        ),
    )(
        queries,
        probes.reshape(pair_count, 1),
        passages,
        centroids,
        counts.astype(jnp.float32).reshape(1, local_count),
    )
    return scores.reshape(per_device, probe_count, span), visits[0, :per_device]


def solution(mesh):
    in_specs = (
        P(("groups", "owner"), None),
        P(("groups", "owner"), None),
        P("owner", None, None),
        P("owner", None),
        P("owner"),
    )
    out_specs = (P(("groups", "owner"), None, None), P(("groups", "owner")))
    return jax.shard_map(body, mesh=mesh, in_specs=in_specs, out_specs=out_specs, check_vma=False)
```

time: 202 us -> 95 us (0.47)
  Pallas kernels: 18.8 us -> 89.6 us
  starting transfers between devices: 64.6 us -> 0 us
  waiting for transfers between devices: 51.3 us -> 0 us
  local copies, waits for them, and re-layouts: 47.5 us -> 3.85 us
  other arithmetic: 18 us -> 0.66 us
    pallas_call x0 -> x1, Pallas kernels: none -> 89.6 us  [body(): pl.pallas_call(functools.partial(kernel, side, cap), out_shape=(jax.Shape...]
    all_to_all x4 -> x0, starting transfers between devices: 64.6 us -> none  [the longest x1 27.4 us: body(): lax.all_to_all(send_ids.reshape(owner_count, capacity), 'owner', split_ax...]
    all_to_all x4 -> x0, waiting for transfers between devices: 51.3 us -> none  [the longest x1 25.6 us: body(): lax.all_to_all(masked_scores.reshape(source_count, slot_count, block_span...]
    gather x7 -> x0, local copies, waits for them, and re-layouts: 30.9 us -> none  [the longest x1 6.87 us: body(): send_ids = jnp.where(slot_filled, target_local[source_pair], -1)]
    another operation x1 -> x0, Pallas kernels: 17 us -> none
    unnamed x9 -> x6, local copies, waits for them, and re-layouts: 13.1 us -> 3.22 us
    sort x2 -> x0, other arithmetic: 8.73 us -> none  [the longest x1 4.37 us: body(): order = jnp.argsort(group_ids, stable=True)]
    select_n x9 -> x0, other arithmetic: 3.04 us -> none  [the longest x1 1.62 us: body(): jnp.where(slot_filled[:, None], queries[source_pair // probe_count], jnp....]
  transfers between devices with their start and end apart: 4 -> 0, of which waited for: 3 -> 0; matrix products, arithmetic and copies ran while one was open for 27% -> 0% of each run, Pallas kernels for 9% -> 0%
where the time goes in v1:
time: 95 us; the launch traced here: 94.8 us
  Pallas kernels  89.6 us (94%)
  local copies, waits for them, and re-layouts  3.85 us (4%)
    pallas_call x1, Pallas kernels, body(): pl.pallas_call(functools.partial(kernel, side, cap), out_shape=(jax.Shape...  89.6 us
    unnamed x6, local copies, waits for them, and re-layouts  3.22 us

profile of v1, /device:TPU:513, one launch (start us, length us, event | category | flops | bytes accessed | tf_op | source)
XLA Modules:
  0.0 94.8 jit_solution(5492147985514269712)
XLA Ops:
  0.6 0.7 convert_bitcast_fusion.cnt_ref
  1.3 0.8 copy.8
  2.1 0.1 reshape.16.pcol_ref
  2.2 0.0 copy-start
  2.2 0.9 copy-done
  3.1 0.0 copy-start.1
  3.1 0.8 copy-done.1
  3.9 89.6 %shard_map.68 = (f32[512,256]{1,0:T(8,128)S(1)}, s32[1,128]{1,0:T(1,128)S(1)}) custom-call(bf16[64,1024]{1,0:T(8,128)(2,1)S(1)} %copy-done, s32[512,1]{1,0:T(8,128)S(1)} %reshape.16.pcol_ref, bf16[16,256,1024]{2,1,0:T(8,128)(2,1)} %pass_hbm.1, bf16[16,1024]{1,0:T(8,128)(2,1)S(1)} %copy-done.1, f32[1,16]{1,0:T(1,128)S(1)} %convert_bitcast_fusion.cnt_ref), custom_call_target="tpu_custom_call" | custom-call | tf_op jit(solution)/shard_map/pallas_call | solution.py:342
  93.5 0.5 slice_bitcast_fusion
  94.0 0.8 copy.11
Async XLA Ops:
  2.2 0.9 copy-start
  3.1 0.8 copy-start.1

commit v2 on v1

--- a/solution.py
+++ b/solution.py
@@ -11,6 +11,10 @@
 MESH = pl.DeviceIdType.MESH
 LANES = 128
 CODE_TOP = 32767.0
+ORDER = (
+    "B0", "P", "B1", "B2", "X0", "S0", "B3", "X1", "S1", "G0", "X2", "S2",
+    "G1", "X3", "G2", "S3", "G3", "F0", "F1", "F2", "F3",
+)
 
 
 def iota(shape, dim):
@@ -19,18 +23,29 @@
 
 def shift_of(t):
     return (2 * lax.rem(t, 2) - 1) * lax.div(t + 1, 2)
+
+
+def shift_int(t):
+    return (t + 1) // 2 * (1 if t % 2 else -1)
+
+
+def number_of(shift, side):
+    return next(t for t in range(side) if (shift_int(t) - shift) % side == 0)
 
 
 def kernel(
     side,
     cap,
     q_hbm,
-    pcol_ref,
+    probe_hbm,
     pass_hbm,
+    cent_hbm,
+    cnt_hbm,
+    out_ref,
+    vis_ref,
+    probe_ref,
     cent_ref,
     cnt_ref,
-    out_ref,
-    vis_ref,
     gq,
     gcode,
     snd,
@@ -46,6 +61,7 @@
     tgt,
     slot_ref,
     load_sem,
+    small_sem,
     pass_sem,
     gq_send,
     gq_recv,
@@ -66,8 +82,8 @@
     y = lax.div(me, 2 * side)
     local_count, span, width = pv.shape
     per_device = gq.shape[1]
-    pair_count = pcol_ref.shape[0]
-    probe_count = pair_count // per_device
+    probe_count = probe_ref.shape[0]
+    pair_count = per_device * probe_count
     owner_count = side * side * 2
     pairs = side // 2
     dests = side * 2
@@ -76,35 +92,47 @@
     def wrap(v):
         return lax.rem(v + side, side)
 
-    def device(first, second, cls, dest_core):
-        yy = wrap(y + second * (1 - cls) + first * cls)
-        xx = wrap(x + first * (1 - cls) + second * cls)
-        return {"owner": (yy * side + xx) * 2 + dest_core}
+    ys = [wrap(y + shift_int(t)) * (2 * side) for t in range(side)]
+    xs = [wrap(x + shift_int(t)) * 2 for t in range(side)]
+    on_first = [(1 - core) * (ys[0] + xs[t]) + core * (ys[t] + xs[0]) for t in range(side)]
+    on_second = [(1 - core) * (ys[t] + xs[0]) + core * (ys[0] + xs[t]) for t in range(side)]
+    mirror = [number_of(-shift_int(t), side) for t in range(side)]
+
+    def at(index):
+        return {"owner": index}
 
     def remote(src, dst, send, recv, dev):
         return pltpu.make_async_remote_copy(
             src_ref=src, dst_ref=dst, send_sem=send, recv_sem=recv, device_id=dev, device_id_type=MESH
         )
 
+    small = [
+        pltpu.make_async_copy(src, dst, small_sem.at[n])
+        for n, (src, dst) in enumerate(((probe_hbm, probe_ref), (cent_hbm, cent_ref), (cnt_hbm, cnt_ref)))
+    ]
+    for copy in small:
+        copy.start()
     own_q = pltpu.make_async_copy(q_hbm, gq.at[0], load_sem)
     own_q.start()
     own_p = pltpu.make_async_copy(pass_hbm, pv, pass_sem)
-    own_p.start()
 
     barrier = pltpu.get_barrier_semaphore()
 
-    def greet(t, carry):
+    for t in range(1, side):
         for dest_core in range(2):
-            for axis in range(2):
-                pl.semaphore_signal(
-                    barrier, inc=1, device_id=device(0, shift_of(t), axis, dest_core), device_id_type=MESH
-                )
-        return carry
-
-    lax.fori_loop(1, side, greet, 0)
-    pl.semaphore_signal(barrier, inc=1, device_id=device(0, 0, 0, 1 - core), device_id_type=MESH)
-
-    pcol = pcol_ref[...]
+            for index in (ys[t] + xs[0], ys[0] + xs[t]):
+                pl.semaphore_signal(barrier, inc=1, device_id=at(index + dest_core), device_id_type=MESH)
+    partner = ys[0] + xs[0] + 1 - core
+    pl.semaphore_signal(barrier, inc=1, device_id=at(partner), device_id_type=MESH)
+
+    for copy in small:
+        copy.wait()
+    by_query = jnp.transpose(probe_ref[...].astype(jnp.float32))
+    spread = jnp.broadcast_to(by_query[:, None, :], (per_device, probe_count, probe_count))
+    chosen = iota((pair_count, probe_count), 1) == lax.rem(iota((pair_count, probe_count), 0), probe_count)
+    pcol = jnp.sum(
+        jnp.where(chosen, spread.reshape(pair_count, probe_count), 0.0), axis=1, keepdims=True
+    ).astype(jnp.int32)
     owner_col = lax.div(pcol, local_count)
     hits = (owner_col == iota((pair_count, owner_count), 1)).astype(jnp.float32)
     earlier = (iota((pair_count, pair_count), 0) > iota((pair_count, pair_count), 1)).astype(jnp.float32)
@@ -128,31 +156,63 @@
     mine = lax.rem(lax.div(row, cap), 2) == lax.div(iota((rows, LANES), 1), per_device)
     tgt[...] = jnp.where(mine, row_slot, -1)
 
-    own_q.wait()
-    pl.semaphore_wait(barrier, 4 * (side - 1) + 1)
-
-    def share(t, carry):
-        dev = device(shift_of(t), 0, core, core)
-        remote(gcode.at[0], gcode.at[t], gc_send.at[t], gc_recv.at[t], dev).start()
-        remote(gq.at[0], gq.at[t], gq_send.at[t], gq_recv.at[t], dev).start()
-        return carry
-
-    lax.fori_loop(1, side, share, 0)
-
+    with jax.named_scope("load"):
+        own_q.wait()
+    with jax.named_scope("barrier"):
+        pl.semaphore_wait(barrier, 4 * (side - 1) + 1)
+
+    def code_to(t):
+        return remote(gcode.at[0], gcode.at[t], gc_send.at[t], gc_recv.at[t], at(on_first[t] + core))
+
+    half = per_device // 2
+
+    def along(distance):
+        return at(on_first[number_of(distance, side)] + core)
+
+    def hop(t):
+        if t < 5:
+            return [remote(gq.at[0], gq.at[t], gq_send.at[t], gq_recv.at[t], along(shift_int(t)))]
+        if t < side - 1:
+            return [remote(gq.at[t - 2], gq.at[t], gq_send.at[t], gq_recv.at[t], along(1 if t % 2 else -1))]
+        parts = []
+        for n, (src, step) in enumerate(((t - 4, 2), (t - 3, -2))):
+            here = pl.ds(n * half, half)
+            parts.append(remote(gq.at[src, here], gq.at[t, here], gq_send.at[t + n], gq_recv.at[t], along(step)))
+        return parts
+
+    for t in (1, 2, 3, 4):
+        for copy in hop(t):
+            copy.start()
+    for t in range(1, side):
+        code_to(t).start()
     def to_owner(p, f, dest_core):
-        dev = device(0, shift_of(f), core, dest_core)
+        dev = at(on_second[f] + dest_core)
         d = f * 2 + dest_core
         return (
             remote(snd.at[p, d], rcv.at[p, f * 2 + core], x_send.at[p], x_recv.at[p], dev),
             remote(scid.at[p, d], rcid.at[p, f * 2 + core], c_send.at[p], c_recv.at[p], dev),
         )
 
-    for p in range(pairs):
+    def whole(ref, sem):
+        return pltpu.make_async_copy(ref, ref, sem)
+
+    def come(t):
+        whole(gq.at[t], gq_recv.at[t]).wait()
+        if t == 3:
+            hop(5)[0].start()
+            hop(7)[0].start()
+        if t == 4:
+            hop(6)[0].start()
+            hop(7)[1].start()
+
+    def arrived(p):
+        for t in ((), (1,), (2, 3, 4), (5,), (6, 7))[p + 1]:
+            come(t)
         for t in (2 * p, 2 * p + 1):
             if t:
-                dev = device(0, 0, core, core)
-                remote(gcode.at[0], gcode.at[t], gc_send.at[t], gc_recv.at[t], dev).wait_recv()
-                remote(gq.at[0], gq.at[t], gq_send.at[t], gq_recv.at[t], dev).wait_recv()
+                code_to(t).wait_recv()
+
+    def build(p):
         code = jnp.where(iota((probe_count, LANES), 1) < per_device, gcode[2 * p], gcode[2 * p + 1])
         slot_of = lax.div(code, local_count)
         mark_of = (lax.rem(code, local_count) + 1).astype(jnp.float32)
@@ -172,30 +232,25 @@
         for d in range(dests):
             scid[p, d] = marks[d : d + 1, :]
 
+    def send(p):
         self_x = pltpu.make_async_copy(snd.at[p, core], rcv.at[p, core], x_recv.at[p])
         self_c = pltpu.make_async_copy(scid.at[p, core], rcid.at[p, core], c_recv.at[p])
         self_c.start()
         self_x.start()
+        for f in range(side - 1, 0, -1):
+            for dest_core in range(2):
+                for copy in to_owner(p, f, dest_core):
+                    copy.start()
         for copy in to_owner(p, 0, 1 - core):
             copy.start()
 
-        def post(f, carry):
-            for dest_core in range(2):
-                a, b = to_owner(p, f, dest_core)
-                b.start()
-                a.start()
-            return carry
-
-        lax.fori_loop(1, side, post, 0)
-
-    def whole(ref, sem):
-        return pltpu.make_async_copy(ref, ref, sem)
-
-    own_p.wait()
-
     def back(p, f, cls, i):
         t = 2 * p + i
-        dev = device(-shift_of(t), -shift_of(f), cls, cls)
+        a, b = mirror[t], mirror[f]
+        if f + t:
+            dev = at((ys[a] + xs[b] if cls else ys[b] + xs[a]) + cls)
+        else:
+            dev = at(partner)
         b = (f * 2 + cls) * 2 + i
         land = (f * 2 + core) * 2 + i
         return (
@@ -203,9 +258,7 @@
             remote(rs.at[p, b], ret.at[p, land], b_send.at[p], b_recv.at[p], dev),
         )
 
-    for p in range(pairs):
-        whole(rcid.at[p], c_recv.at[p]).wait()
-        whole(rcv.at[p], x_recv.at[p]).wait()
+    def score(p):
         row = iota((rows, LANES), 0)
         lane = iota((rows, LANES), 1)
         seen = jnp.broadcast_to(rcid[p], (dests, 2 * cap, LANES)).reshape(rows, LANES)
@@ -223,7 +276,7 @@
             acc[...] = jnp.where(cid == c, got, acc[...])
             return carry
 
-        lax.fori_loop(0, local_count, cluster, 0)
+        lax.fori_loop(0, local_count, cluster, 0, unroll=8)
         centres = lax.dot_general(
             rcv[p].reshape(rows, width),
             cent_ref[...],
@@ -232,7 +285,7 @@
         )
         of_row = iota((rows, local_count), 1) == cid
         centre = jnp.sum(jnp.where(of_row, centres, 0.0), axis=1, keepdims=True)
-        live = jnp.sum(jnp.where(of_row, cnt_ref[...], 0.0), axis=1, keepdims=True)
+        live = jnp.sum(jnp.where(of_row, cnt_ref[...].astype(jnp.float32), 0.0), axis=1, keepdims=True)
         within = iota((rows, span), 1).astype(jnp.float32) < live
         value = jnp.where(within, acc[...] + centre, 0.0)
         top = jnp.maximum(jnp.max(jnp.abs(value), axis=1, keepdims=True), 1e-30)
@@ -240,40 +293,31 @@
         low, high = coded[:, : span // 2], coded[:, span // 2 :]
         rs[p] = (high * 65536 + (low & 65535)).reshape(dests * 2, cap, LANES)
         spot = lax.rem(lane, cap) == lax.rem(row, cap)
-        scales = jnp.sum(
-            jnp.where(spot, top * (1.0 / CODE_TOP), 0.0).reshape(dests * 2, cap, LANES), axis=1
-        )
-        lives = jnp.sum(jnp.where(spot, live, 0.0).reshape(dests * 2, cap, LANES), axis=1)
-        both = jnp.concatenate([scales, lives], axis=1)
+        even = lax.rem(lax.div(lane, cap), 2) == 0
+        both = jnp.where(even, top * (1.0 / CODE_TOP), live)
+        both = jnp.sum(jnp.where(spot, both, 0.0).reshape(dests * 2, cap, LANES), axis=1)
         for b in range(dests * 2):
             sm[p, b] = both[b : b + 1, :]
 
-        def give(f, carry):
-            for cls in range(2):
-                for i in range(2):
-                    for copy in back(p, f, cls, i):
-                        copy.start()
-            return carry
-
+    def give_all(p):
+        for f in range(side - 1, -1, -1):
+            for i in (1, 0):
+                for cls in range(2):
+                    if f + p + i:
+                        for copy in back(p, f, cls, i):
+                            copy.start()
         if p == 0:
             self_b = core * 2
             pltpu.make_async_copy(sm.at[0, self_b], rmeta.at[0, self_b], m_recv.at[0]).start()
             pltpu.make_async_copy(rs.at[0, self_b], ret.at[0, self_b], b_recv.at[0]).start()
             for copy in back(0, 0, 1 - core, 0):
                 copy.start()
-            for cls in range(2):
-                for copy in back(0, 0, cls, 1):
-                    copy.start()
-            lax.fori_loop(1, side, give, 0)
-        else:
-            lax.fori_loop(0, side, give, 0)
 
     scale_col = jnp.zeros((pair_count, 1), jnp.float32)
     live_col = jnp.zeros((pair_count, 1), jnp.float32)
-    slots = slot_ref[...]
-    for p in range(pairs):
-        whole(rmeta.at[p], m_recv.at[p]).wait()
-        whole(ret.at[p], b_recv.at[p]).wait()
+
+    def finish(p, scale_col, live_col):
+        slots = slot_ref[...]
         spot_lane = iota((1, rows), 1)
         block = lax.div(spot_lane, cap)
         second = shift_of(lax.div(block, 4))
@@ -300,24 +344,50 @@
         scale_lane, live_lane = [], []
         for h in range(rows // LANES):
             meta = jnp.concatenate([rmeta[p, h * each + b] for b in range(each)], axis=0)
-            keep = lax.div(iota((each, LANES), 1), cap) == iota((each, LANES), 0)
-            scale_lane.append(jnp.sum(jnp.where(keep, meta[:, :LANES], 0.0), axis=0, keepdims=True))
-            live_lane.append(jnp.sum(jnp.where(keep, meta[:, LANES:], 0.0), axis=0, keepdims=True))
+            group, block = lax.div(iota((each, LANES), 1), cap), iota((each, LANES), 0)
+            twin = block + 1 - 2 * lax.rem(block, 2)
+            here = jnp.sum(jnp.where(group == block, meta, 0.0), axis=0, keepdims=True)
+            there = jnp.sum(jnp.where(group == twin, meta, 0.0), axis=0, keepdims=True)
+            even = lax.rem(lax.div(iota((1, LANES), 1), cap), 2) == 0
+            scale_lane.append(jnp.where(even, here, pltpu.roll(there, cap, 1)))
+            live_lane.append(jnp.where(even, pltpu.roll(there, LANES - cap, 1), here))
         scale_col += jnp.sum(
             jnp.where(match, jnp.concatenate(scale_lane, axis=1), 0.0), axis=1, keepdims=True
         )
         live_col += jnp.sum(jnp.where(match, jnp.concatenate(live_lane, axis=1), 0.0), axis=1, keepdims=True)
+        return scale_col, live_col
+
+    for step in ORDER:
+        kind, p = step[0], int(step[1:] or 0)
+        with jax.named_scope(step):
+            if kind == "B":
+                arrived(p)
+                build(p)
+                send(p)
+            if kind == "P":
+                own_p.start()
+            if kind == "X":
+                whole(rcid.at[p], c_recv.at[p]).wait()
+                whole(rcv.at[p], x_recv.at[p]).wait()
+            if kind == "S":
+                if p == 0:
+                    own_p.wait()
+                score(p)
+            if kind == "G":
+                give_all(p)
+            if kind == "F":
+                whole(rmeta.at[p], m_recv.at[p]).wait()
+                whole(ret.at[p], b_recv.at[p]).wait()
+                scale_col, live_col = finish(p, scale_col, live_col)
+
     out_ref[...] = out_ref[...] * scale_col
-    at_query = iota((pair_count, LANES), 1) == lax.div(iota((pair_count, LANES), 0), probe_count)
+    at_query = iota((pair_count, per_device), 1) == lax.div(iota((pair_count, per_device), 0), probe_count)
     vis_ref[...] = jnp.sum(jnp.where(at_query, live_col, 0.0), axis=0, keepdims=True).astype(jnp.int32)
 
-    def sent(t, carry):
-        dev = device(shift_of(t), 0, core, core)
-        remote(gcode.at[0], gcode.at[t], gc_send.at[t], gc_recv.at[t], dev).wait_send()
-        remote(gq.at[0], gq.at[t], gq_send.at[t], gq_recv.at[t], dev).wait_send()
-        return carry
-
-    lax.fori_loop(1, side, sent, 0)
+    for t in range(1, side):
+        code_to(t).wait_send()
+        for copy in hop(t):
+            copy.wait_send()
     for p in range(pairs):
         whole(snd.at[p, pl.ds(0, dests - 1)], x_send.at[p]).wait()
         whole(scid.at[p, pl.ds(0, dests - 1)], c_send.at[p]).wait()
@@ -337,17 +407,20 @@
     dests = side * 2
     rows = dests * 2 * cap
     vmem = pl.BlockSpec(memory_space=pltpu.VMEM)
-    hbm = pl.BlockSpec(memory_space=pl.ANY)
+    hbm = pl.BlockSpec(memory_space=pltpu.HBM)
     dma = pltpu.SemaphoreType.DMA
     scores, visits = pl.pallas_call(
         functools.partial(kernel, side, cap),
         out_shape=(
             jax.ShapeDtypeStruct((pair_count, span), jnp.float32),
-            jax.ShapeDtypeStruct((1, LANES), jnp.int32),
+            jax.ShapeDtypeStruct((1, per_device), jnp.int32),
         ),
-        in_specs=[hbm, vmem, hbm, vmem, vmem],
+        in_specs=[hbm] * 5,
         out_specs=(vmem, vmem),
         scratch_shapes=[
+            pltpu.VMEM((probe_count, per_device), jnp.int32),
+            pltpu.VMEM((local_count, width), jnp.bfloat16),
+            pltpu.VMEM((1, local_count), jnp.int32),
             pltpu.VMEM((side, per_device, width), jnp.bfloat16),
             pltpu.VMEM((side, probe_count, LANES), jnp.int32),
             pltpu.VMEM((pairs, dests, 2 * cap, width), jnp.bfloat16),
@@ -356,18 +429,19 @@
             pltpu.VMEM((pairs, dests, 1, LANES), jnp.float32),
             pltpu.VMEM((rows, span), jnp.float32),
             pltpu.VMEM((pairs, dests * 2, cap, LANES), jnp.int32),
-            pltpu.VMEM((pairs, dests * 2, 1, 2 * LANES), jnp.float32),
+            pltpu.VMEM((pairs, dests * 2, 1, LANES), jnp.float32),
             pltpu.VMEM((pairs, dests * 2, cap, LANES), jnp.int32),
-            pltpu.VMEM((pairs, dests * 2, 1, 2 * LANES), jnp.float32),
+            pltpu.VMEM((pairs, dests * 2, 1, LANES), jnp.float32),
             pltpu.VMEM((local_count, span, width), jnp.bfloat16),
             pltpu.VMEM((rows, LANES), jnp.int32),
             pltpu.VMEM((pair_count, 1), jnp.int32),
             dma,
+            dma((3,)),
             dma,
+            dma((side + 1,)),
             dma((side,)),
             dma((side,)),
             dma((side,)),
-            dma((side,)),
             dma((pairs,)),
             dma((pairs,)),
             dma((pairs,)),
@@ -378,16 +452,16 @@
             dma((pairs,)),
         ],
         compiler_params=pltpu.CompilerParams(
-            collective_id=0, has_side_effects=True, vmem_limit_bytes=48 * 1024 * 1024
+            collective_id=0, has_side_effects=True, vmem_limit_bytes=60 * 1024 * 1024
         ),
     )(
         queries,
-        probes.reshape(pair_count, 1),
+        probes.T,
         passages,
         centroids,
-        counts.astype(jnp.float32).reshape(1, local_count),
+        counts.reshape(1, local_count),
     )
-    return scores.reshape(per_device, probe_count, span), visits[0, :per_device]
+    return scores.reshape(per_device, probe_count, span), visits.reshape(per_device)
 
 
 def solution(mesh):

time: 95 us -> 77.9 us (0.82)
  Pallas kernels: 89.6 us -> 73.5 us
    pallas_call x1, Pallas kernels: 89.6 us -> 73.5 us  [body(): pl.pallas_call(functools.partial(kernel, side, cap), out_shape=(jax.Shape...]
    unnamed x6 -> x2, local copies, waits for them, and re-layouts: 3.22 us -> 2.97 us
where the time goes in v2:
time: 77.9 us; the launch traced here: 77.1 us
  Pallas kernels  73.5 us (94%)
  local copies, waits for them, and re-layouts  2.97 us (4%)
    pallas_call x1, Pallas kernels, body(): pl.pallas_call(functools.partial(kernel, side, cap), out_shape=(jax.Shape...  73.5 us
    unnamed x2, local copies, waits for them, and re-layouts  2.97 us

profile of v2, /device:TPU:513, one launch (start us, length us, event | category | flops | bytes accessed | tf_op | source)
XLA Modules:
  0.0 77.1 jit_solution(15884567101423268099)
XLA Ops:
  0.6 73.5 %shard_map.68 = (f32[512,256]{1,0:T(8,128)}, s32[1,64]{1,0:T(1,128)}) custom-call(bf16[64,1024]{1,0:T(8,128)(2,1)} %q_hbm.1, s32[8,64]{1,0:T(8,128)} %bitcast.5, bf16[16,256,1024]{2,1,0:T(8,128)(2,1)} %pass_hbm.1, bf16[16,1024]{1,0:T(8,128)(2,1)} %cent_hbm.1, s32[1,16]{1,0:T(1,128)} %bitcast.6), custom_call_target="tpu_custom_call" | custom-call | tf_op jit(solution)/shard_map/pallas_call | solution.py:412
  74.1 1.9 %copy.9 = f32[64,8,256]{2,1,0:T(8,128)} copy(f32[64,8,256]{2,1,0:T(8,128)} %bitcast.4) | data formatting | bytes 1048576
  76.0 1.1 %copy.10 = s32[64]{0:T(128)} copy(s32[64]{0:T(128)} %bitcast.7) | data formatting | bytes 512

commit v3 on v2

--- a/solution.py
+++ b/solution.py
@@ -11,9 +11,10 @@
 MESH = pl.DeviceIdType.MESH
 LANES = 128
 CODE_TOP = 32767.0
+LEVELS, LEVEL_BASE, COUNT_BASE = 32.0, 8192.0, 512.0
 ORDER = (
-    "B0", "P", "B1", "B2", "X0", "S0", "B3", "X1", "S1", "G0", "X2", "S2",
-    "G1", "X3", "G2", "S3", "G3", "F0", "F1", "F2", "F3",
+    "B0", "P", "B1", "T0", "T1", "B2", "T2", "T3", "X0", "S0", "B3", "X1", "S1", "G0",
+    "X2", "S2", "G1", "X30", "G2", "S30", "G30", "X31", "S31", "G31", "F0", "F1", "F2", "F3",
 )
 
 
@@ -54,10 +55,9 @@
     rcid,
     acc,
     rs,
-    sm,
     ret,
-    rmeta,
     pv,
+    pvt,
     tgt,
     slot_ref,
     load_sem,
@@ -73,8 +73,6 @@
     c_recv,
     b_send,
     b_recv,
-    m_send,
-    m_recv,
 ):
     me = lax.axis_index("owner")
     core = lax.rem(me, 2)
@@ -189,8 +187,8 @@
         dev = at(on_second[f] + dest_core)
         d = f * 2 + dest_core
         return (
-            remote(snd.at[p, d], rcv.at[p, f * 2 + core], x_send.at[p], x_recv.at[p], dev),
-            remote(scid.at[p, d], rcid.at[p, f * 2 + core], c_send.at[p], c_recv.at[p], dev),
+            remote(snd.at[p, d], rcv.at[p, f * 2 + core], x_send.at[p], x_recv.at[p, f // (side // 2)], dev),
+            remote(scid.at[p, d], rcid.at[p, f * 2 + core], c_send.at[p], c_recv.at[p, f // (side // 2)], dev),
         )
 
     def whole(ref, sem):
@@ -233,8 +231,8 @@
             scid[p, d] = marks[d : d + 1, :]
 
     def send(p):
-        self_x = pltpu.make_async_copy(snd.at[p, core], rcv.at[p, core], x_recv.at[p])
-        self_c = pltpu.make_async_copy(scid.at[p, core], rcid.at[p, core], c_recv.at[p])
+        self_x = pltpu.make_async_copy(snd.at[p, core], rcv.at[p, core], x_recv.at[p, 0])
+        self_c = pltpu.make_async_copy(scid.at[p, core], rcid.at[p, core], c_recv.at[p, 0])
         self_c.start()
         self_x.start()
         for f in range(side - 1, 0, -1):
@@ -243,6 +241,8 @@
                     copy.start()
         for copy in to_owner(p, 0, 1 - core):
             copy.start()
+
+    used = pl.ds(0, cap + 1)
 
     def back(p, f, cls, i):
         t = 2 * p + i
@@ -253,32 +253,29 @@
             dev = at(partner)
         b = (f * 2 + cls) * 2 + i
         land = (f * 2 + core) * 2 + i
-        return (
-            remote(sm.at[p, b], rmeta.at[p, land], m_send.at[p], m_recv.at[p], dev),
-            remote(rs.at[p, b], ret.at[p, land], b_send.at[p], b_recv.at[p], dev),
-        )
-
-    def score(p):
+        return remote(rs.at[p, b, used], ret.at[p, land, used], b_send.at[p], b_recv.at[p], dev)
+
+    def score(p, first, count):
+        rows = count * 2 * cap
+        part = pl.ds(first, count)
+        sums = acc.at[pl.ds(0, rows)]
         row = iota((rows, LANES), 0)
         lane = iota((rows, LANES), 1)
-        seen = jnp.broadcast_to(rcid[p], (dests, 2 * cap, LANES)).reshape(rows, LANES)
+        seen = jnp.broadcast_to(rcid[p, part], (count, 2 * cap, LANES)).reshape(rows, LANES)
         cid = jnp.sum(jnp.where(lane == lax.rem(row, 2 * cap), seen, 0.0), axis=1, keepdims=True) - 1.0
         cid = cid.astype(jnp.int32)
-        acc[...] = jnp.zeros_like(acc)
+        sums[...] = jnp.zeros_like(sums)
 
         def cluster(c, carry):
-            got = lax.dot_general(
-                rcv[p].reshape(rows, width),
-                pv[c],
-                (((1,), (1,)), ((), ())),
-                preferred_element_type=jnp.float32,
+            got = jnp.dot(
+                rcv[p, part].reshape(rows, width), pvt[c], preferred_element_type=jnp.float32
             )
-            acc[...] = jnp.where(cid == c, got, acc[...])
+            sums[...] = jnp.where(cid == c, got, sums[...])
             return carry
 
         lax.fori_loop(0, local_count, cluster, 0, unroll=8)
         centres = lax.dot_general(
-            rcv[p].reshape(rows, width),
+            rcv[p, part].reshape(rows, width),
             cent_ref[...],
             (((1,), (1,)), ((), ())),
             preferred_element_type=jnp.float32,
@@ -287,36 +284,33 @@
         centre = jnp.sum(jnp.where(of_row, centres, 0.0), axis=1, keepdims=True)
         live = jnp.sum(jnp.where(of_row, cnt_ref[...].astype(jnp.float32), 0.0), axis=1, keepdims=True)
         within = iota((rows, span), 1).astype(jnp.float32) < live
-        value = jnp.where(within, acc[...] + centre, 0.0)
+        value = jnp.where(within, sums[...] + centre, 0.0)
         top = jnp.maximum(jnp.max(jnp.abs(value), axis=1, keepdims=True), 1e-30)
-        coded = jnp.round(value * (CODE_TOP / top)).astype(jnp.int32)
+        level = jnp.ceil(jnp.log2(top) * LEVELS)
+        coded = jnp.round(value * (CODE_TOP / jnp.exp2(level * (1.0 / LEVELS)))).astype(jnp.int32)
         low, high = coded[:, : span // 2], coded[:, span // 2 :]
-        rs[p] = (high * 65536 + (low & 65535)).reshape(dests * 2, cap, LANES)
+        words = (high * 65536 + (low & 65535)).reshape(count * 2, cap, LANES)
+        rs[p, pl.ds(first * 2, count * 2), pl.ds(0, cap)] = words
         spot = lax.rem(lane, cap) == lax.rem(row, cap)
-        even = lax.rem(lax.div(lane, cap), 2) == 0
-        both = jnp.where(even, top * (1.0 / CODE_TOP), live)
-        both = jnp.sum(jnp.where(spot, both, 0.0).reshape(dests * 2, cap, LANES), axis=1)
-        for b in range(dests * 2):
-            sm[p, b] = both[b : b + 1, :]
-
-    def give_all(p):
-        for f in range(side - 1, -1, -1):
+        both = (level + LEVEL_BASE) * COUNT_BASE + live
+        both = jnp.sum(jnp.where(spot, both, 0.0).reshape(count * 2, cap, LANES), axis=1).astype(jnp.int32)
+        for b in range(count * 2):
+            rs[p, first * 2 + b, pl.ds(cap, 1)] = both[b : b + 1, :]
+
+    def give_all(p, peers):
+        for f in peers:
             for i in (1, 0):
                 for cls in range(2):
                     if f + p + i:
-                        for copy in back(p, f, cls, i):
-                            copy.start()
+                        back(p, f, cls, i).start()
         if p == 0:
             self_b = core * 2
-            pltpu.make_async_copy(sm.at[0, self_b], rmeta.at[0, self_b], m_recv.at[0]).start()
-            pltpu.make_async_copy(rs.at[0, self_b], ret.at[0, self_b], b_recv.at[0]).start()
-            for copy in back(0, 0, 1 - core, 0):
-                copy.start()
-
-    scale_col = jnp.zeros((pair_count, 1), jnp.float32)
-    live_col = jnp.zeros((pair_count, 1), jnp.float32)
-
-    def finish(p, scale_col, live_col):
+            pltpu.make_async_copy(rs.at[0, self_b, used], ret.at[0, self_b, used], b_recv.at[0]).start()
+            back(0, 0, 1 - core, 0).start()
+
+    both_col = jnp.zeros((pair_count, 1), jnp.float32)
+
+    def finish(p, both_col):
         slots = slot_ref[...]
         spot_lane = iota((1, rows), 1)
         block = lax.div(spot_lane, cap)
@@ -327,7 +321,7 @@
         have = ((yy * side + xx) * 2 + lax.rem(lax.div(block, 2), 2)) * cap + lax.rem(spot_lane, cap)
         match = slots == have
         pick = jnp.where(match, 1.0, 0.0).astype(jnp.bfloat16)
-        words = ret[p].reshape(rows, LANES)
+        words = ret[p, :, pl.ds(0, cap)].reshape(rows, LANES)
 
         def piece(low, high):
             return jnp.concatenate([low, high], axis=1).astype(jnp.float32).astype(jnp.bfloat16)
@@ -341,24 +335,28 @@
         )
         out_ref[...] = sums if p == 0 else out_ref[...] + sums
         each = LANES // cap
-        scale_lane, live_lane = [], []
+        both_lane = []
         for h in range(rows // LANES):
-            meta = jnp.concatenate([rmeta[p, h * each + b] for b in range(each)], axis=0)
-            group, block = lax.div(iota((each, LANES), 1), cap), iota((each, LANES), 0)
-            twin = block + 1 - 2 * lax.rem(block, 2)
-            here = jnp.sum(jnp.where(group == block, meta, 0.0), axis=0, keepdims=True)
-            there = jnp.sum(jnp.where(group == twin, meta, 0.0), axis=0, keepdims=True)
-            even = lax.rem(lax.div(iota((1, LANES), 1), cap), 2) == 0
-            scale_lane.append(jnp.where(even, here, pltpu.roll(there, cap, 1)))
-            live_lane.append(jnp.where(even, pltpu.roll(there, LANES - cap, 1), here))
-        scale_col += jnp.sum(
-            jnp.where(match, jnp.concatenate(scale_lane, axis=1), 0.0), axis=1, keepdims=True
-        )
-        live_col += jnp.sum(jnp.where(match, jnp.concatenate(live_lane, axis=1), 0.0), axis=1, keepdims=True)
-        return scale_col, live_col
+            meta = jnp.concatenate([ret[p, h * each + b, pl.ds(cap, 1)] for b in range(each)], axis=0)
+            keep = lax.div(iota((each, LANES), 1), cap) == iota((each, LANES), 0)
+            both_lane.append(jnp.sum(jnp.where(keep, meta.astype(jnp.float32), 0.0), axis=0, keepdims=True))
+        return both_col + jnp.sum(
+            jnp.where(match, jnp.concatenate(both_lane, axis=1), 0.0), axis=1, keepdims=True
+        )
+
+    quarter = local_count // 4
+
+    def turn(n):
+        def one(c, carry):
+            pvt[c] = jnp.transpose(pv[c])
+            return carry
+
+        lax.fori_loop(n * quarter, (n + 1) * quarter, one, 0)
 
     for step in ORDER:
-        kind, p = step[0], int(step[1:] or 0)
+        kind, p = step[0], int(step[1:2] or 0)
+        halves = (int(step[2:]),) if step[2:] else (0, 1)
+        peers = range(halves[0] * (side // 2), (halves[-1] + 1) * (side // 2))
         with jax.named_scope(step):
             if kind == "B":
                 arrived(p)
@@ -366,21 +364,26 @@
                 send(p)
             if kind == "P":
                 own_p.start()
-            if kind == "X":
-                whole(rcid.at[p], c_recv.at[p]).wait()
-                whole(rcv.at[p], x_recv.at[p]).wait()
-            if kind == "S":
+            if kind == "T":
                 if p == 0:
                     own_p.wait()
-                score(p)
+                turn(p)
+            if kind == "X":
+                for h in halves:
+                    here = pl.ds(h * side, side)
+                    whole(rcid.at[p, here], c_recv.at[p, h]).wait()
+                    whole(rcv.at[p, here], x_recv.at[p, h]).wait()
+            if kind == "S":
+                score(p, halves[0] * side, len(halves) * side)
             if kind == "G":
-                give_all(p)
+                give_all(p, peers)
             if kind == "F":
-                whole(rmeta.at[p], m_recv.at[p]).wait()
-                whole(ret.at[p], b_recv.at[p]).wait()
-                scale_col, live_col = finish(p, scale_col, live_col)
-
-    out_ref[...] = out_ref[...] * scale_col
+                whole(ret.at[p, :, used], b_recv.at[p]).wait()
+                both_col = finish(p, both_col)
+
+    level_col = jnp.floor(both_col * (1.0 / COUNT_BASE))
+    live_col = both_col - level_col * COUNT_BASE
+    out_ref[...] = out_ref[...] * (jnp.exp2((level_col - LEVEL_BASE) * (1.0 / LEVELS)) * (1.0 / CODE_TOP))
     at_query = iota((pair_count, per_device), 1) == lax.div(iota((pair_count, per_device), 0), probe_count)
     vis_ref[...] = jnp.sum(jnp.where(at_query, live_col, 0.0), axis=0, keepdims=True).astype(jnp.int32)
 
@@ -392,8 +395,7 @@
         whole(snd.at[p, pl.ds(0, dests - 1)], x_send.at[p]).wait()
         whole(scid.at[p, pl.ds(0, dests - 1)], c_send.at[p]).wait()
         blocks = dests * 2 - (1 if p == 0 else 0)
-        whole(rs.at[p, pl.ds(0, blocks)], b_send.at[p]).wait()
-        whole(sm.at[p, pl.ds(0, blocks)], m_send.at[p]).wait()
+        whole(rs.at[p, pl.ds(0, blocks), used], b_send.at[p]).wait()
 
 
 def body(queries, probes, passages, centroids, counts):
@@ -428,11 +430,10 @@
             pltpu.VMEM((pairs, dests, 2 * cap, width), jnp.bfloat16),
             pltpu.VMEM((pairs, dests, 1, LANES), jnp.float32),
             pltpu.VMEM((rows, span), jnp.float32),
-            pltpu.VMEM((pairs, dests * 2, cap, LANES), jnp.int32),
-            pltpu.VMEM((pairs, dests * 2, 1, LANES), jnp.float32),
-            pltpu.VMEM((pairs, dests * 2, cap, LANES), jnp.int32),
-            pltpu.VMEM((pairs, dests * 2, 1, LANES), jnp.float32),
+            pltpu.VMEM((pairs, dests * 2, 2 * cap, LANES), jnp.int32),
+            pltpu.VMEM((pairs, dests * 2, 2 * cap, LANES), jnp.int32),
             pltpu.VMEM((local_count, span, width), jnp.bfloat16),
+            pltpu.VMEM((local_count, width, span), jnp.bfloat16),
             pltpu.VMEM((rows, LANES), jnp.int32),
             pltpu.VMEM((pair_count, 1), jnp.int32),
             dma,
@@ -443,11 +444,9 @@
             dma((side,)),
             dma((side,)),
             dma((pairs,)),
+            dma((pairs, 2)),
             dma((pairs,)),
-            dma((pairs,)),
-            dma((pairs,)),
-            dma((pairs,)),
-            dma((pairs,)),
+            dma((pairs, 2)),
             dma((pairs,)),
             dma((pairs,)),
         ],

time: 77.9 us -> 77.2 us (level)
  no operation moved by 1% of the time
where the time goes in v3:
time: 77.2 us; the launch traced here: 76.8 us
  Pallas kernels  73.1 us (95%)
  local copies, waits for them, and re-layouts  2.97 us (4%)
    pallas_call x1, Pallas kernels, body(): pl.pallas_call(functools.partial(kernel, side, cap), out_shape=(jax.Shape...  73.1 us
    unnamed x2, local copies, waits for them, and re-layouts  2.97 us

profile of v3, /device:TPU:513, one launch (start us, length us, event | category | flops | bytes accessed | tf_op | source)
XLA Modules:
  0.0 76.8 jit_solution(7303236492826800235)
XLA Ops:
  0.6 73.1 %shard_map.68 = (f32[512,256]{1,0:T(8,128)}, s32[1,64]{1,0:T(1,128)}) custom-call(bf16[64,1024]{1,0:T(8,128)(2,1)} %q_hbm.1, s32[8,64]{1,0:T(8,128)} %bitcast.5, bf16[16,256,1024]{2,1,0:T(8,128)(2,1)} %pass_hbm.1, bf16[16,1024]{1,0:T(8,128)(2,1)} %cent_hbm.1, s32[1,16]{1,0:T(1,128)} %bitcast.6), custom_call_target="tpu_custom_call" | custom-call | tf_op jit(solution)/shard_map/pallas_call | solution.py:414
  73.8 1.9 %copy.9 = f32[64,8,256]{2,1,0:T(8,128)} copy(f32[64,8,256]{2,1,0:T(8,128)} %bitcast.4) | data formatting | bytes 1048576
  75.7 1.1 %copy.10 = s32[64]{0:T(128)} copy(s32[64]{0:T(128)} %bitcast.7) | data formatting | bytes 512
